TPU v7x, 128 devices: a whole 4x4x4 slice. The times are simulated.
128 devices in a mesh: fsdp: 32 (over y, z_lo, x), tp: 4 (over z_hi, core).
Axes of the slice: x: 4, y: 4, z: 4 (z_hi: 2, z_lo: 2; z = z_hi * 2 + z_lo), core: 2. Of those that a mesh axis runs over, the one named last changes fastest.
Arguments:
- partials: bfloat16 [32, 2, 5120, 1024], P('fsdp', None, None, 'tp'), may hold values from -6 to 6
- token_counts: int32 [32], P('fsdp'), may hold values from 100 to 599
- owner_map: int32 [2, 4], replicated, may hold values from 0 to 3, each once within a row
- params: float32 [2, 5120, 1024], P(None, 'fsdp', 'tp'), may hold values from -0.75 to 0.75
- moment1: float32 [2, 5120, 1024], P(None, 'fsdp', 'tp'), may hold values from -0.15625 to 0.15625
- moment2: float32 [2, 5120, 1024], P(None, 'fsdp', 'tp'), may hold values from 0.0001 to 0.004
Outputs:
- new_params: float32 [2, 5120, 1024], P(None, 'fsdp', 'tp')
- new_moment1: float32 [2, 5120, 1024], P(None, 'fsdp', 'tp')
- new_moment2: float32 [2, 5120, 1024], P(None, 'fsdp', 'tp')
- rollout_delta: bfloat16 [2, 5120, 1024], P(None, None, 'tp')
Inputs may be any that keep to these rules, and one draw needn't show every extreme that they name: `owner_map`: each row is a permutation of 0 to 3.
All inputs are finite; a program needn't handle non-finite values.
Results may differ from a plain program's by a relative error of at most 0.0004.
Values may be sent and summed in bfloat16 or wider, within the bound.
A program may use at most 64 MiB of HBM per device.

v0:
```python
import jax
import jax.numpy as jnp
from jax import lax
from jax.sharding import Mesh
from jax.sharding import PartitionSpec as P

STEP = 10
FSDP = ("fsdp_0", "fsdp_1", "fsdp_2")


def sent_to_all(value, axis):
    peers = lax.axis_size(axis)
    return lax.all_to_all(
        jnp.broadcast_to(value[None], (peers, *value.shape)), axis, 0, 0, tiled=True
    )


def over_copies(value, axis):
    everything = sent_to_all(value, axis)
    return jnp.sum(everything, axis=0)


def joined_along(tiles, dim):
    tiles = jnp.moveaxis(tiles, 0, dim)
    dims = tiles.shape
    return tiles.reshape(*dims[:dim], dims[dim] * dims[dim + 1], *dims[dim + 2 :])


def collect(value, axis, dim):
    return joined_along(sent_to_all(value, axis), dim)


def all_blocks(value, axes, order):
    tiles = value[None]
    for k in order:
        tiles = lax.all_gather(tiles, axes[k], axis=0, tiled=True)
    carried = [lax.axis_size(axes[k]) for k in reversed(order)]
    tiles = tiles.reshape(*carried, *value.shape)
    turned = sorted(range(len(order)), key=lambda place: order[len(order) - 1 - place])
    return tiles.transpose(*turned, *range(len(order), tiles.ndim)).reshape(-1, *value.shape)


def whole_of(value, axes, order, dim):
    return joined_along(all_blocks(value, axes, order), dim)


def local(partials, token_counts, owner_map, params, moment1, moment2):
    weight = token_counts.astype(jnp.float32)[0]
    total = over_copies(weight, FSDP)
    counts = collect(token_counts, FSDP, 0).astype(jnp.float32)
    arrived = lax.all_to_all(partials, FSDP, split_axis=2, concat_axis=0, tiled=True)
    summed = jnp.sum(counts[:, None, None, None] * arrived.astype(jnp.float32), axis=0)
    grad = summed / total
    first = 0.9 * moment1 + 0.1 * grad
    second = 0.999 * moment2 + 0.001 * grad * grad
    bias_one = 1.0 - 0.9**STEP
    bias_two = 1.0 - 0.999**STEP
    direction = first / bias_one / (jnp.sqrt(second / bias_two) + 1e-08)
    new_params = params - 0.001 * (direction + 0.1 * params)
    delta = direction.astype(jnp.bfloat16)
    owners = lax.axis_size("tp")
    column = lax.axis_index("tp")
    served = lax.dynamic_index_in_dim(owner_map, column, 1, keepdims=False)
    select = served[:, None] == jnp.arange(owners, dtype=jnp.int32)[None, :]
    wide = collect(delta, "tp", 2)
    block = wide.shape[2] // owners
    split = wide.reshape(wide.shape[0], wide.shape[1], owners, block)
    kept = jnp.where(select[:, None, :, None], split, jnp.zeros((), jnp.bfloat16))
    rollout = whole_of(jnp.sum(kept, axis=2), FSDP, (1, 0, 2), 1)
    return (new_params, first, second, rollout)


def solution(mesh):
    split = Mesh(
        mesh.devices.reshape(4, 2, 4, mesh.shape["tp"]), ("fsdp_0", "fsdp_1", "fsdp_2", "tp")
    )
    return jax.shard_map(
        local,
        mesh=split,
        in_specs=(
            P(FSDP, None, None, "tp"),
            P(FSDP),
            P(),
            P(None, FSDP, "tp"),
            P(None, FSDP, "tp"),
            P(None, FSDP, "tp"),
        ),
        out_specs=(
            P(None, FSDP, "tp"),
            P(None, FSDP, "tp"),
            P(None, FSDP, "tp"),
            P(None, None, "tp"),
        ),
        check_vma=False,
    )
```

profile of v0, /device:TPU:1, one launch (start us, length us, event | category | flops | bytes accessed | tf_op | source)
XLA Modules:
  0.0 245.0 jit_solution(1411335727446816097)
XLA Ops:
  7.2 0.0 copy-start
  7.8 0.6 broadcast_in_dim.41
  8.5 9.2 %all-to-all-start = ((s32[32,1,1]{2,1,0:T(1,128)}), s32[32,1,1]{2,1,0:T(1,128)S(1)}, u32[]{:S(2)}, u32[]{:S(2)}) async-start(s32[32,1,1]{2,1,0:T(1,128)} %broadcast_in_dim.41), calls=%async_computation | async-start | bytes 32768 | tf_op jit(solution)/shard_map/all_to_all | solution.py:13
  17.7 7.1 %all-to-all-done = s32[32,1,1]{2,1,0:T(1,128)S(1)} async-done(((s32[32,1,1]{2,1,0:T(1,128)}), s32[32,1,1]{2,1,0:T(1,128)S(1)}, u32[]{:S(2)}, u32[]{:S(2)}) %all-to-all-start) | async-done | bytes 160 | tf_op jit(solution)/shard_map/all_to_all | solution.py:13
  24.8 0.6 broadcast_in_dim.43
  25.4 3.8 %all-to-all-start.2 = ((f32[32,1,1]{2,1,0:T(1,128)}), f32[32,1,1]{2,1,0:T(1,128)S(1)}, u32[]{:S(2)}, u32[]{:S(2)}) async-start(f32[32,1,1]{2,1,0:T(1,128)} %broadcast_in_dim.43), calls=%async_computation.2 | async-start | bytes 32768 | tf_op jit(solution)/shard_map/all_to_all | solution.py:13
  29.2 10.8 %copy.53 = bf16[1,2,5120,256]{3,1,0,2:T(2,128)(2,1)} copy(bf16[1,2,5120,256]{3,2,1,0:T(8,128)(2,1)} %param.6) | data formatting | bytes 10485760 | tf_op args[0]
  40.1 0.0 all-to-all-done.2
  40.1 7.8 %all-to-all-start.1 = ((bf16[1,2,5120,256]{3,1,0,2:T(2,128)(2,1)}), bf16[1,2,5120,256]{3,1,0,2:T(2,128)(2,1)}, u32[]{:S(2)}, u32[]{:S(2)}) async-start(bf16[1,2,5120,256]{3,1,0,2:T(2,128)(2,1)} %copy.53), calls=%async_computation.1 | async-start | bytes 10485760 | tf_op jit(solution)/shard_map/all_to_all | solution.py:51
  47.9 0.0 copy-start.4
  47.9 0.0 copy-start.5
  47.9 0.6 reduce_sum.31
  48.6 0.3 convert_reduce_fusion
  48.9 62.3 %all-to-all-done.1 = bf16[1,2,5120,256]{3,1,0,2:T(2,128)(2,1)} async-done(((bf16[1,2,5120,256]{3,1,0,2:T(2,128)(2,1)}), bf16[1,2,5120,256]{3,1,0,2:T(2,128)(2,1)}, u32[]{:S(2)}, u32[]{:S(2)}) %all-to-all-start.1) | async-done | bytes 5242912 | tf_op jit(solution)/shard_map/all_to_all | solution.py:51
  111.2 0.0 copy-start.3
  111.2 8.3 %fusion = f32[2,160,256]{2,0,1:T(2,128)S(1)} fusion(bf16[1,2,32,160,256]{4,1,3,2,0:T(2,128)(2,1)} %bitcast.12, f32[32]{0:T(128)S(1)} %convert_reduce_fusion), kind=kLoop, calls=%fused_computation.1 | loop fusion | flops 7782400 | bytes 5570688 | tf_op jit(solution)/shard_map/reduce_sum | solution.py:52
  119.4 0.0 copy-done.4
  119.4 0.0 copy-done.5
  119.5 0.9 fusion.3
  120.3 0.0 copy-start.1
  120.4 0.0 copy-start.2
  120.4 1.0 broadcast_in_dim.45
  121.4 6.2 %all-to-all-start.3 = ((bf16[4,2,160,256]{3,2,1,0:T(8,128)(2,1)}), bf16[4,2,160,256]{3,2,1,0:T(8,128)(2,1)S(1)}, u32[]{:S(2)}, u32[]{:S(2)}) async-start(bf16[4,2,160,256]{3,2,1,0:T(8,128)(2,1)} %broadcast_in_dim.45), calls=%async_computation.3 | async-start | bytes 1310720 | tf_op jit(solution)/shard_map/all_to_all | solution.py:13
  127.6 0.0 all-gather.4.cloned.1.call-start
  127.6 0.0 copy-done
  127.6 0.2 dynamic-slice_reduce_fusion
  127.8 10.6 %all-to-all-done.3 = bf16[4,2,160,256]{3,2,1,0:T(8,128)(2,1)S(1)} async-done(((bf16[4,2,160,256]{3,2,1,0:T(8,128)(2,1)}), bf16[4,2,160,256]{3,2,1,0:T(8,128)(2,1)S(1)}, u32[]{:S(2)}, u32[]{:S(2)}) %all-to-all-start.3) | async-done | bytes 655392 | tf_op jit(solution)/shard_map/all_to_all | solution.py:13
  138.3 0.1 fusion.1
  138.5 5.6 %all-gather = bf16[4,160,256]{2,1,0:T(8,128)(2,1)} all-gather(bf16[2,160,256]{2,1,0:T(8,128)(2,1)S(1)} %fusion.1), channel_id=2, replica_groups=mesh['fsdp_0'=4,'fsdp_1'=2,'fsdp_2'=4,'tp'=4] {'fsdp_1'}, dimensions={0}, use_global_device_ids=true | all-gather | bytes 491520 | tf_op jit(solution)/shard_map/all_gather | solution.py:36
  144.0 0.0 all-gather.4.cloned.1.call-update
  144.1 0.0 all-gather.6.cloned.1.call-start
  144.1 28.3 %all-gather.4.cloned.1.call-done = bf16[8,2,160,256]{3,2,1,0:T(8,128)(2,1)} async-done(((bf16[2,2,160,256]{3,2,1,0:T(8,128)(2,1)}), bf16[8,2,160,256]{3,2,1,0:T(8,128)(2,1)}) %all-gather.4.cloned.1.call-update) | async-done | bytes 1310736 | tf_op jit(solution)/shard_map/all_gather | solution.py:36
  172.4 0.0 all-gather.6.cloned.1.call-update
  172.4 0.0 copy-done.3
  172.4 0.9 multiply_subtract_fusion
  173.4 59.1 %all-gather.6.cloned.1.call-done = bf16[32,2,160,256]{3,2,1,0:T(8,128)(2,1)} async-done(((bf16[8,2,160,256]{3,2,1,0:T(8,128)(2,1)}), bf16[32,2,160,256]{3,2,1,0:T(8,128)(2,1)}) %all-gather.6.cloned.1.call-update) | async-done | bytes 5242896 | tf_op jit(solution)/shard_map/all_gather | solution.py:36
  232.5 2.9 %copy.56 = bf16[4,2,4,2,160,256]{5,4,3,2,1,0:T(8,128)(2,1)S(1)} copy(bf16[4,2,4,2,160,256]{5,4,3,1,0,2:T(8,128)(2,1)} %bitcast.24) | data formatting | bytes 10485760 | tf_op jit(solution)/shard_map/transpose | solution.py:40
  235.3 0.0 copy-done.1
  235.3 0.0 copy-done.2
  235.4 2.8 %copy.57 = bf16[2,32,160,256]{3,2,1,0:T(8,128)(2,1)} copy(bf16[2,32,160,256]{3,2,0,1:T(8,128)(2,1)S(1)} %bitcast.23) | data formatting | bytes 10485760 | tf_op jit(solution)/shard_map/transpose | solution.py:24
  (1 shorter events, 0.0 us)
Async XLA Ops:
  7.2 120.4 %copy-start = (s32[2,4]{1,0:T(2,128)S(1)}, s32[2,4]{1,0:T(2,128)}, u32[]{:S(2)}) copy-start(s32[2,4]{1,0:T(2,128)} %param.8) | copy-start | bytes 100
  8.5 16.3 %all-to-all-start = ((s32[32,1,1]{2,1,0:T(1,128)}), s32[32,1,1]{2,1,0:T(1,128)S(1)}, u32[]{:S(2)}, u32[]{:S(2)}) async-start(s32[32,1,1]{2,1,0:T(1,128)} %broadcast_in_dim.41), calls=%async_computation | async-start | bytes 32768 | tf_op jit(solution)/shard_map/all_to_all | solution.py:13
  25.4 14.7 %all-to-all-start.2 = ((f32[32,1,1]{2,1,0:T(1,128)}), f32[32,1,1]{2,1,0:T(1,128)S(1)}, u32[]{:S(2)}, u32[]{:S(2)}) async-start(f32[32,1,1]{2,1,0:T(1,128)} %broadcast_in_dim.43), calls=%async_computation.2 | async-start | bytes 32768 | tf_op jit(solution)/shard_map/all_to_all | solution.py:13
  40.1 71.1 %all-to-all-start.1 = ((bf16[1,2,5120,256]{3,1,0,2:T(2,128)(2,1)}), bf16[1,2,5120,256]{3,1,0,2:T(2,128)(2,1)}, u32[]{:S(2)}, u32[]{:S(2)}) async-start(bf16[1,2,5120,256]{3,1,0,2:T(2,128)(2,1)} %copy.53), calls=%async_computation.1 | async-start | bytes 10485760 | tf_op jit(solution)/shard_map/all_to_all | solution.py:51
  47.9 71.5 %copy-start.4 = (f32[2,160,256]{2,1,0:T(8,128)S(1)}, f32[2,160,256]{2,1,0:T(8,128)}, u32[]{:S(2)}) copy-start(f32[2,160,256]{2,1,0:T(8,128)} %param.10) | copy-start | bytes 983044
  47.9 71.5 %copy-start.5 = (f32[2,160,256]{2,1,0:T(8,128)S(1)}, f32[2,160,256]{2,1,0:T(8,128)}, u32[]{:S(2)}) copy-start(f32[2,160,256]{2,1,0:T(8,128)} %param.11) | copy-start | bytes 983044
  111.2 61.3 %copy-start.3 = (f32[2,160,256]{2,1,0:T(8,128)S(1)}, f32[2,160,256]{2,1,0:T(8,128)}, u32[]{:S(2)}) copy-start(f32[2,160,256]{2,1,0:T(8,128)} %param.9) | copy-start | bytes 983044
  120.3 115.0 %copy-start.1 = (f32[2,160,256]{2,1,0:T(8,128)}, f32[2,160,256]{2,1,0:T(8,128)S(1)}, u32[]{:S(2)}) copy-start(f32[2,160,256]{2,1,0:T(8,128)S(1)} %get-tuple-element.17) | copy-start | bytes 983044
  120.4 115.0 %copy-start.2 = (f32[2,160,256]{2,1,0:T(8,128)}, f32[2,160,256]{2,1,0:T(8,128)S(1)}, u32[]{:S(2)}) copy-start(f32[2,160,256]{2,1,0:T(8,128)S(1)} %get-tuple-element.18) | copy-start | bytes 983044
  121.4 17.0 %all-to-all-start.3 = ((bf16[4,2,160,256]{3,2,1,0:T(8,128)(2,1)}), bf16[4,2,160,256]{3,2,1,0:T(8,128)(2,1)S(1)}, u32[]{:S(2)}, u32[]{:S(2)}) async-start(bf16[4,2,160,256]{3,2,1,0:T(8,128)(2,1)} %broadcast_in_dim.45), calls=%async_computation.3 | async-start | bytes 1310720 | tf_op jit(solution)/shard_map/all_to_all | solution.py:13
  127.6 44.8 %all-gather.4.cloned.1.call-start = ((), (), s32[]{:S(2)}) async-start(), calls=%async_computation.4 | async-start | bytes 1638400 | tf_op jit(solution)/shard_map/all_gather | solution.py:36
  144.1 88.4 %all-gather.6.cloned.1.call-start = ((), (), s32[]{:S(2)}) async-start(), calls=%async_computation.5 | async-start | bytes 6553600 | tf_op jit(solution)/shard_map/all_gather | solution.py:36
Sparse Core Ops, SparseCore 0:
  144.2 28.1 all-gather.3
  174.1 58.3 all-gather.5
where the time goes:
time: 245 us
  waiting for transfers between devices  167 us (68%)
  starting transfers between devices  27.2 us (11%)
  local copies, waits for them, and re-layouts  18.9 us (8%)
  between operations  14.8 us (6%)
  other arithmetic  11.1 us (5%)
  blocking collectives  5.55 us (2%)
    all_gather x2, waiting for transfers between devices, all_blocks(): tiles = lax.all_gather(tiles, axes[k], axis=0, tiled=True)  87.4 us
    all_to_all x1, waiting for transfers between devices, local(): lax.all_to_all(partials, FSDP, split_axis=2, concat_axis=0, tiled=True)  62.3 us
    all_to_all x3, starting transfers between devices, sent_to_all(): lax.all_to_all(jnp.broadcast_to(value[None], (peers, *value.shape)), axis...  19.3 us
    all_to_all x3, waiting for transfers between devices, sent_to_all(): lax.all_to_all(jnp.broadcast_to(value[None], (peers, *value.shape)), axis...  17.6 us
    unnamed x13, local copies, waits for them, and re-layouts  10.9 us
    reduce_sum x1, other arithmetic, local(): jnp.sum(counts[:, None, None, None] * arrived.astype(jnp.float32), axis=0)  8.25 us
    all_to_all x1, starting transfers between devices, local(): lax.all_to_all(partials, FSDP, split_axis=2, concat_axis=0, tiled=True)  7.85 us
    all_gather x1, blocking collectives, all_blocks(): tiles = lax.all_gather(tiles, axes[k], axis=0, tiled=True)  5.55 us
  transfers between devices with their start and end apart: 6, of which 5 were waited for; matrix products, arithmetic and copies ran while one was open for 5% of the time, Pallas kernels for 0%

commit v1 on v0

--- a/solution.py
+++ b/solution.py
@@ -33,7 +33,13 @@
 def all_blocks(value, axes, order):
     tiles = value[None]
     for k in order:
-        tiles = lax.all_gather(tiles, axes[k], axis=0, tiled=True)
+        slab_in = axes[k]
+        tiles = jnp.concatenate(
+            lax.all_to_all(
+                jnp.stack(lax.axis_size(slab_in) * [tiles]), slab_in, split_axis=0, concat_axis=0
+            ),
+            0,
+        )
     carried = [lax.axis_size(axes[k]) for k in reversed(order)]
     tiles = tiles.reshape(*carried, *value.shape)
     turned = sorted(range(len(order)), key=lambda place: order[len(order) - 1 - place])

time: 245 us -> 237 us (0.967); the launches traced: 245 us -> 233 us
  waiting for transfers between devices: 167 us -> 136 us
  blocking collectives: 5.55 us -> 28.8 us
  between operations: 14.8 us -> 1.44 us
  starting transfers between devices: 27.2 us -> 33.6 us
  local copies, waits for them, and re-layouts: 18.9 us -> 22.3 us
    all_gather x2 -> x0, waiting for transfers between devices: 87.4 us -> none  [all_blocks(): tiles = lax.all_gather(tiles, axes[k], axis=0, tiled=True)]
    all_to_all x0 -> x1, waiting for transfers between devices: none -> 55.8 us  [all_blocks(): lax.all_to_all(jnp.stack(lax.axis_size(slab_in) * [tiles]), slab_in, spli...]
    all_to_all x0 -> x2, blocking collectives: none -> 28.8 us  [all_blocks(): lax.all_to_all(jnp.stack(lax.axis_size(slab_in) * [tiles]), slab_in, spli...]
    all_to_all x0 -> x1, starting transfers between devices: none -> 6.52 us  [all_blocks(): lax.all_to_all(jnp.stack(lax.axis_size(slab_in) * [tiles]), slab_in, spli...]
    all_gather x1 -> x0, blocking collectives: 5.55 us -> none  [all_blocks(): tiles = lax.all_gather(tiles, axes[k], axis=0, tiled=True)]
    another operation x0 -> x4, local copies, waits for them, and re-layouts: none -> 3.23 us  [all_blocks(): jnp.stack(lax.axis_size(slab_in) * [tiles])]
    all_to_all x0 -> x2, local copies, waits for them, and re-layouts: none -> 3.03 us  [all_blocks(): lax.all_to_all(jnp.stack(lax.axis_size(slab_in) * [tiles]), slab_in, spli...]
    transpose x1 -> x0, local copies, waits for them, and re-layouts: 2.86 us -> none  [all_blocks(): tiles.transpose(*turned, *range(len(order), tiles.ndim))]
  transfers between devices with their start and end apart: 6 -> 5, of which waited for: 5 -> 4; matrix products, arithmetic and copies ran while one was open for 5% -> 6% of each run, Pallas kernels for 0% -> 0%
where the time goes in v1:
time: 237 us; the launch traced here: 233 us
  waiting for transfers between devices  136 us (57%)
  starting transfers between devices  33.6 us (14%)
  blocking collectives  28.8 us (12%)
  local copies, waits for them, and re-layouts  22.3 us (9%)
  other arithmetic  11.1 us (5%)
    all_to_all x1, waiting for transfers between devices, local(): lax.all_to_all(partials, FSDP, split_axis=2, concat_axis=0, tiled=True)  62.3 us
    all_to_all x1, waiting for transfers between devices, all_blocks(): lax.all_to_all(jnp.stack(lax.axis_size(slab_in) * [tiles]), slab_in, spli...  55.8 us
    all_to_all x2, blocking collectives, all_blocks(): lax.all_to_all(jnp.stack(lax.axis_size(slab_in) * [tiles]), slab_in, spli...  28.8 us
    all_to_all x3, starting transfers between devices, sent_to_all(): lax.all_to_all(jnp.broadcast_to(value[None], (peers, *value.shape)), axis...  19.3 us
    all_to_all x3, waiting for transfers between devices, sent_to_all(): lax.all_to_all(jnp.broadcast_to(value[None], (peers, *value.shape)), axis...  17.7 us
    unnamed x13, local copies, waits for them, and re-layouts  10.9 us
    reduce_sum x1, other arithmetic, local(): jnp.sum(counts[:, None, None, None] * arrived.astype(jnp.float32), axis=0)  8.22 us
    all_to_all x1, starting transfers between devices, local(): lax.all_to_all(partials, FSDP, split_axis=2, concat_axis=0, tiled=True)  7.85 us
  transfers between devices with their start and end apart: 5, of which 4 were waited for; matrix products, arithmetic and copies ran while one was open for 6% of the time, Pallas kernels for 0%

profile of v1, /device:TPU:1, one launch (start us, length us, event | category | flops | bytes accessed | tf_op | source)
XLA Modules:
  0.0 233.0 jit_solution(18400594791987795196)
XLA Ops:
  0.6 0.0 copy-start
  1.3 0.6 broadcast_in_dim.38
  1.9 9.2 %all-to-all-start = ((s32[32,1,1]{2,1,0:T(1,128)}), s32[32,1,1]{2,1,0:T(1,128)S(1)}, u32[]{:S(2)}, u32[]{:S(2)}) async-start(s32[32,1,1]{2,1,0:T(1,128)} %broadcast_in_dim.38), calls=%async_computation | async-start | bytes 32768 | tf_op jit(solution)/shard_map/all_to_all | solution.py:13
  11.1 7.1 %all-to-all-done = s32[32,1,1]{2,1,0:T(1,128)S(1)} async-done(((s32[32,1,1]{2,1,0:T(1,128)}), s32[32,1,1]{2,1,0:T(1,128)S(1)}, u32[]{:S(2)}, u32[]{:S(2)}) %all-to-all-start) | async-done | bytes 160 | tf_op jit(solution)/shard_map/all_to_all | solution.py:13
  18.2 0.6 broadcast_in_dim.40
  18.9 3.8 %all-to-all-start.2 = ((f32[32,1,1]{2,1,0:T(1,128)}), f32[32,1,1]{2,1,0:T(1,128)S(1)}, u32[]{:S(2)}, u32[]{:S(2)}) async-start(f32[32,1,1]{2,1,0:T(1,128)} %broadcast_in_dim.40), calls=%async_computation.2 | async-start | bytes 32768 | tf_op jit(solution)/shard_map/all_to_all | solution.py:13
  22.7 10.8 %copy.66 = bf16[1,2,5120,256]{3,1,0,2:T(2,128)(2,1)} copy(bf16[1,2,5120,256]{3,2,1,0:T(8,128)(2,1)} %param.6) | data formatting | bytes 10485760 | tf_op args[0]
  33.5 0.0 all-to-all-done.2
  33.5 7.8 %all-to-all-start.1 = ((bf16[1,2,5120,256]{3,1,0,2:T(2,128)(2,1)}), bf16[1,2,5120,256]{3,1,0,2:T(2,128)(2,1)}, u32[]{:S(2)}, u32[]{:S(2)}) async-start(bf16[1,2,5120,256]{3,1,0,2:T(2,128)(2,1)} %copy.66), calls=%async_computation.1 | async-start | bytes 10485760 | tf_op jit(solution)/shard_map/all_to_all | solution.py:57
  41.4 0.0 copy-start.4
  41.4 0.0 copy-start.5
  41.4 0.6 reduce_sum.31
  42.0 0.3 convert_reduce_fusion
  42.4 62.3 %all-to-all-done.1 = bf16[1,2,5120,256]{3,1,0,2:T(2,128)(2,1)} async-done(((bf16[1,2,5120,256]{3,1,0,2:T(2,128)(2,1)}), bf16[1,2,5120,256]{3,1,0,2:T(2,128)(2,1)}, u32[]{:S(2)}, u32[]{:S(2)}) %all-to-all-start.1) | async-done | bytes 5242912 | tf_op jit(solution)/shard_map/all_to_all | solution.py:57
  104.6 8.2 %fusion = f32[2,160,256]{2,0,1:T(2,128)S(1)} fusion(bf16[1,2,32,160,256]{4,1,3,2,0:T(2,128)(2,1)} %bitcast.14, f32[32]{0:T(128)S(1)} %convert_reduce_fusion), kind=kLoop, calls=%fused_computation.1 | loop fusion | flops 7782400 | bytes 5570688 | tf_op jit(solution)/shard_map/reduce_sum | solution.py:58
  112.9 0.0 copy-done.4
  112.9 0.0 copy-done.5
  112.9 0.9 fusion.3
  113.8 0.0 copy-start.1
  113.8 0.0 copy-start.2
  113.8 1.0 broadcast_in_dim.42
  114.8 6.2 %all-to-all-start.3 = ((bf16[4,2,160,256]{3,2,1,0:T(8,128)(2,1)}), bf16[4,2,160,256]{3,2,1,0:T(8,128)(2,1)S(1)}, u32[]{:S(2)}, u32[]{:S(2)}) async-start(bf16[4,2,160,256]{3,2,1,0:T(8,128)(2,1)} %broadcast_in_dim.42), calls=%async_computation.3 | async-start | bytes 1310720 | tf_op jit(solution)/shard_map/all_to_all | solution.py:13
  121.0 0.0 copy-done
  121.0 0.2 dynamic-slice_reduce_fusion
  121.2 10.6 %all-to-all-done.3 = bf16[4,2,160,256]{3,2,1,0:T(8,128)(2,1)S(1)} async-done(((bf16[4,2,160,256]{3,2,1,0:T(8,128)(2,1)}), bf16[4,2,160,256]{3,2,1,0:T(8,128)(2,1)S(1)}, u32[]{:S(2)}, u32[]{:S(2)}) %all-to-all-start.3) | async-done | bytes 655392 | tf_op jit(solution)/shard_map/all_to_all | solution.py:13
  131.8 0.1 fusion.1
  131.9 7.1 %all_to_all.41 = bf16[2,1,2,160,256]{4,3,2,1,0:T(8,128)(2,1)S(1)} all-to-all(bf16[2,1,2,160,256]{4,3,2,1,0:T(8,128)(2,1)S(1)} %pad_maximum_fusion), channel_id=1, replica_groups=mesh['fsdp_0'=4,'fsdp_1'=2,'fsdp_2'=4,'tp'=4] {'fsdp_1'}, dimensions={0} | all-to-all | bytes 655360 | tf_op jit(solution)/shard_map/all_to_all | solution.py:38
  139.1 0.1 stack.10
  139.3 21.7 %all_to_all.42 = bf16[4,2,2,160,256]{4,3,1,2,0:T(8,128)(2,1)S(1)} all-to-all(bf16[4,2,2,160,256]{4,3,1,2,0:T(8,128)(2,1)S(1)} %stack.10), channel_id=1, replica_groups=mesh['fsdp_0'=4,'fsdp_1'=2,'fsdp_2'=4,'tp'=4] {'fsdp_0'}, dimensions={0} | all-to-all | bytes 2621440 | tf_op jit(solution)/shard_map/all_to_all | solution.py:38
  160.9 0.1 copy.70
  161.0 0.1 copy.71
  161.1 3.0 %stack.11 = bf16[4,8,2,160,256]{4,3,1,2,0:T(8,128)(2,1)} broadcast(bf16[8,2,160,256]{3,2,0,1:T(8,128)(2,1)S(1)} %copy.71), dimensions={1,2,3,4} | broadcast | bytes 6553600 | tf_op jit(solution)/shard_map/stack | solution.py:39
  164.1 0.0 copy-start.3
  164.1 6.5 %all-to-all-start.6 = ((bf16[4,8,2,160,256]{4,3,1,2,0:T(8,128)(2,1)}), bf16[4,8,2,160,256]{4,3,1,2,0:T(8,128)(2,1)}, u32[]{:S(2)}, u32[]{:S(2)}) async-start(bf16[4,8,2,160,256]{4,3,1,2,0:T(8,128)(2,1)} %stack.11), calls=%async_computation.6 | async-start | bytes 10485760 | tf_op jit(solution)/shard_map/all_to_all | solution.py:38
  170.6 0.0 copy-done.1
  170.6 0.0 copy-done.2
  170.6 0.0 copy-done.3
  170.6 0.9 multiply_subtract_fusion
  171.5 55.8 %all-to-all-done.6 = bf16[4,8,2,160,256]{4,3,1,2,0:T(8,128)(2,1)} async-done(((bf16[4,8,2,160,256]{4,3,1,2,0:T(8,128)(2,1)}), bf16[4,8,2,160,256]{4,3,1,2,0:T(8,128)(2,1)}, u32[]{:S(2)}, u32[]{:S(2)}) %all-to-all-start.6) | async-done | bytes 5242912 | tf_op jit(solution)/shard_map/all_to_all | solution.py:38
  227.3 2.9 %copy.72 = bf16[4,8,2,160,256]{4,3,2,0,1:T(8,128)(2,1)S(1)} copy(bf16[4,8,2,160,256]{4,3,1,2,0:T(8,128)(2,1)} %all-to-all-done.6) | data formatting | bytes 10485760 | tf_op jit(solution)/shard_map/all_to_all | solution.py:38
  230.3 2.8 %copy.73 = bf16[2,32,160,256]{3,2,1,0:T(8,128)(2,1)} copy(bf16[2,32,160,256]{3,2,0,1:T(8,128)(2,1)S(1)} %bitcast.26) | data formatting | bytes 10485760 | tf_op jit(solution)/shard_map/transpose | solution.py:24
  (3 shorter events, 0.1 us)
Async XLA Ops:
  0.6 120.4 %copy-start = (s32[2,4]{1,0:T(2,128)S(1)}, s32[2,4]{1,0:T(2,128)}, u32[]{:S(2)}) copy-start(s32[2,4]{1,0:T(2,128)} %param.8) | copy-start | bytes 100
  1.9 16.3 %all-to-all-start = ((s32[32,1,1]{2,1,0:T(1,128)}), s32[32,1,1]{2,1,0:T(1,128)S(1)}, u32[]{:S(2)}, u32[]{:S(2)}) async-start(s32[32,1,1]{2,1,0:T(1,128)} %broadcast_in_dim.38), calls=%async_computation | async-start | bytes 32768 | tf_op jit(solution)/shard_map/all_to_all | solution.py:13
  18.9 14.7 %all-to-all-start.2 = ((f32[32,1,1]{2,1,0:T(1,128)}), f32[32,1,1]{2,1,0:T(1,128)S(1)}, u32[]{:S(2)}, u32[]{:S(2)}) async-start(f32[32,1,1]{2,1,0:T(1,128)} %broadcast_in_dim.40), calls=%async_computation.2 | async-start | bytes 32768 | tf_op jit(solution)/shard_map/all_to_all | solution.py:13
  33.5 71.1 %all-to-all-start.1 = ((bf16[1,2,5120,256]{3,1,0,2:T(2,128)(2,1)}), bf16[1,2,5120,256]{3,1,0,2:T(2,128)(2,1)}, u32[]{:S(2)}, u32[]{:S(2)}) async-start(bf16[1,2,5120,256]{3,1,0,2:T(2,128)(2,1)} %copy.66), calls=%async_computation.1 | async-start | bytes 10485760 | tf_op jit(solution)/shard_map/all_to_all | solution.py:57
  41.4 71.5 %copy-start.4 = (f32[2,160,256]{2,1,0:T(8,128)S(1)}, f32[2,160,256]{2,1,0:T(8,128)}, u32[]{:S(2)}) copy-start(f32[2,160,256]{2,1,0:T(8,128)} %param.10) | copy-start | bytes 983044
  41.4 71.5 %copy-start.5 = (f32[2,160,256]{2,1,0:T(8,128)S(1)}, f32[2,160,256]{2,1,0:T(8,128)}, u32[]{:S(2)}) copy-start(f32[2,160,256]{2,1,0:T(8,128)} %param.11) | copy-start | bytes 983044
  113.8 56.9 %copy-start.1 = (f32[2,160,256]{2,1,0:T(8,128)}, f32[2,160,256]{2,1,0:T(8,128)S(1)}, u32[]{:S(2)}) copy-start(f32[2,160,256]{2,1,0:T(8,128)S(1)} %get-tuple-element.17) | copy-start | bytes 983044
  113.8 56.8 %copy-start.2 = (f32[2,160,256]{2,1,0:T(8,128)}, f32[2,160,256]{2,1,0:T(8,128)S(1)}, u32[]{:S(2)}) copy-start(f32[2,160,256]{2,1,0:T(8,128)S(1)} %get-tuple-element.18) | copy-start | bytes 983044
  114.8 17.0 %all-to-all-start.3 = ((bf16[4,2,160,256]{3,2,1,0:T(8,128)(2,1)}), bf16[4,2,160,256]{3,2,1,0:T(8,128)(2,1)S(1)}, u32[]{:S(2)}, u32[]{:S(2)}) async-start(bf16[4,2,160,256]{3,2,1,0:T(8,128)(2,1)} %broadcast_in_dim.42), calls=%async_computation.3 | async-start | bytes 1310720 | tf_op jit(solution)/shard_map/all_to_all | solution.py:13
  164.1 6.5 %copy-start.3 = (f32[2,160,256]{2,1,0:T(8,128)S(1)}, f32[2,160,256]{2,1,0:T(8,128)}, u32[]{:S(2)}) copy-start(f32[2,160,256]{2,1,0:T(8,128)} %param.9) | copy-start | bytes 983044
  164.1 63.2 %all-to-all-start.6 = ((bf16[4,8,2,160,256]{4,3,1,2,0:T(8,128)(2,1)}), bf16[4,8,2,160,256]{4,3,1,2,0:T(8,128)(2,1)}, u32[]{:S(2)}, u32[]{:S(2)}) async-start(bf16[4,8,2,160,256]{4,3,1,2,0:T(8,128)(2,1)} %stack.11), calls=%async_computation.6 | async-start | bytes 10485760 | tf_op jit(solution)/shard_map/all_to_all | solution.py:38
